TPU v7x, 256 devices: a whole 4x4x8 slice. The times are simulated.
256 devices in a mesh: batch: 4 (over x), heads: 64 (over y, z, core).
Axes of the slice: x: 4, y: 4, z: 8, core: 2. Of those that a mesh axis runs over, the one named last changes fastest.
Arguments:
- draft_ids: int32 [192, 8], P('batch'), may hold values from 0 to 50279
- accepted: int32 [192], P('batch'), may hold values from 1 to 8
- embedding: bfloat16 [50280, 2560], P(None, 'heads'), may hold values from -6 to 6
- norm_gain: float32 [2, 2560], replicated, may hold values from 0.5 to 1.5
- w_zx: bfloat16 [2, 2560, 64, 128], P(None, None, 'heads'), may hold values from -0.125 to 0.125
- w_dt: bfloat16 [2, 2560, 64], P(None, None, 'heads'), may hold values from -0.125 to 0.125
- w_bc: bfloat16 [2, 2560, 256], P(None, None, 'heads'), may hold values from -0.125 to 0.125
- dt_bias: float32 [2, 64], P(None, 'heads'), may hold values from -4 to -1
- decay_rate: float32 [2, 64], P(None, 'heads'), may hold values from 1 to 16
- skip_weight: float32 [2, 64], P(None, 'heads'), may hold values from 0.5 to 1.5
- conv_x_w: bfloat16 [2, 4, 4096], P(None, None, 'heads'), may hold values from -3 to 3
- conv_x_b: bfloat16 [2, 4096], P(None, 'heads'), may hold values from -3 to 3
- conv_bc_w: bfloat16 [2, 4, 256], P(None, None, 'heads'), may hold values from -3 to 3
- conv_bc_b: bfloat16 [2, 256], P(None, 'heads'), may hold values from -3 to 3
- gate_gain: float32 [2, 4096], P(None, 'heads'), may hold values from 0.5 to 1.5
- out_w: bfloat16 [2, 4096, 2560], P(None, 'heads'), may hold values from -0.25 to 0.25
- ssm_state: float32 [2, 192, 64, 64, 128], P(None, 'batch', 'heads'), may hold values from -1.6 to 1.6
- conv_x_state: bfloat16 [2, 192, 3, 4096], P(None, 'batch', None, 'heads'), may hold values from -6 to 6
- conv_bc_state: bfloat16 [2, 192, 3, 256], P(None, 'batch', None, 'heads'), may hold values from -6 to 6
Outputs:
- hidden_out: bfloat16 [1536, 2560], P('batch', 'heads')
- new_ssm: float32 [2, 192, 64, 64, 128], P(None, 'batch', 'heads')
- new_conv_x: bfloat16 [2, 192, 3, 4096], P(None, 'batch', None, 'heads')
- new_conv_bc: bfloat16 [2, 192, 3, 256], P(None, 'batch', None, 'heads')
Inputs may be any that keep to these rules, and one draw needn't show every extreme that they name: `accepted`: the number of a sequence's draft tokens that are kept, counted from the first.
All inputs are finite; a program needn't handle non-finite values.
Results may differ from a plain program's by a relative error of at most 0.015.
Values may be sent and summed in bfloat16 or wider, within the bound.
No kernel may reach another device: no remote copies, remote signals or barrier semaphores. Data moves between devices by JAX's collectives and lax.ppermute only.
A program may use at most 128 MiB of HBM per device.

v0:
```python
import jax
import jax.numpy as jnp
from jax import lax
from jax.sharding import PartitionSpec as P

LAYERS = 2
EPS = 1e-05


def turned_gather(arrays, axis, dims):
    turned = [jnp.moveaxis(a, dim, 0) for a, dim in zip(arrays, dims)]
    widths = [t[0].size for t in turned]
    both = jnp.concatenate([t.reshape(-1, w) for t, w in zip(turned, widths)], axis=1)
    filled = lax.all_gather(both, axis, axis=0, tiled=True)
    blocks = jnp.split(filled, [sum(widths[:k]) for k in range(1, len(widths))], axis=1)
    return tuple(
        (
            jnp.moveaxis(b.reshape(-1, *t.shape[1:]), 0, dim)
            for b, t, dim in zip(blocks, turned, dims)
        )
    )


def in_order(blocks, dim):
    blocks = jnp.moveaxis(blocks, 0, dim)
    dims = blocks.shape
    return blocks.reshape(*dims[:dim], dims[dim] * dims[dim + 1], *dims[dim + 2 :])


def sent_to_all(value, axis):
    count = lax.axis_size(axis)
    return lax.all_to_all(
        jnp.broadcast_to(value[None], (count, *value.shape)), axis, 0, 0, tiled=True
    )


def gather_directly(value, axis, dim):
    return in_order(sent_to_all(value, axis), dim)


def rms_scale(total, count):
    return lax.rsqrt(total / count + EPS)


def convolve(window, weight, bias, count):
    weight = weight.astype(jnp.float32)
    acc = window[:, 0:count] * weight[0]
    for k in range(1, weight.shape[0]):
        acc = acc + window[:, k : k + count] * weight[k]
    return jax.nn.silu(acc + bias.astype(jnp.float32))


def keep_rows(window, accepted, kept_rows):
    last_start = window.shape[1] - kept_rows
    kept = window[:, 1 : 1 + kept_rows]
    for start in range(2, last_start + 1):
        kept = jnp.where(
            (accepted == start)[:, None, None], window[:, start : start + kept_rows], kept
        )
    return kept


def recur(decay, step, values, bmat, cmat, skip, state, accepted):
    kept = state
    outputs = []
    for t in range(values.shape[1]):
        state = (
            decay[:, t, None, None] * state
            + (step[:, t, None] * values[:, t])[:, :, None] * bmat[:, t, None, :]
        )
        outputs.append(jnp.sum(state * cmat[:, t, None, :], axis=-1) + skip * values[:, t])
        kept = jnp.where((accepted == t + 1)[:, None, None], state, kept)
    return (jnp.stack(outputs, 1), kept)


def local(
    draft_ids,
    accepted,
    embedding,
    norm_gain,
    w_zx,
    w_dt,
    w_bc,
    dt_bias,
    decay_rate,
    skip_weight,
    conv_x_w,
    conv_x_b,
    conv_bc_w,
    conv_bc_b,
    gate_gain,
    out_w,
    ssm_state,
    conv_x_state,
    conv_bc_state,
):
    seq_rows, draft = draft_ids.shape
    heads_here = w_zx.shape[2]
    width = w_zx.shape[3] // 2
    local_inner = heads_here * width
    own_cols = embedding.shape[1]
    model = own_cols * lax.axis_size("heads")
    inner = local_inner * lax.axis_size("heads")
    bc_here = w_bc.shape[2]
    kernel = conv_x_w.shape[1]
    recur_heads = jax.vmap(recur, in_axes=(2, 2, 2, None, None, 0, 1, None), out_axes=(2, 1))
    whole_bc = turned_gather((w_bc, conv_bc_w, conv_bc_b, conv_bc_state), "heads", (2, 2, 1, 3))
    saved_state, saved_x, saved_bc = ([], [], [])

    def mixer(layer, stream):
        value = stream.astype(jnp.float32)
        normed = (
            value * rms_scale(jnp.sum(value * value, -1, keepdims=True), model) * norm_gain[layer]
        ).astype(jnp.bfloat16)
        zx = jnp.dot(
            normed, w_zx[layer].reshape(model, -1), preferred_element_type=jnp.float32
        ).astype(jnp.bfloat16)
        zx = zx.reshape(seq_rows, draft, heads_here, 2, width)
        gate_z = zx[:, :, :, 0].astype(jnp.float32)
        values = zx[:, :, :, 1].reshape(seq_rows, draft, local_inner)
        dt_raw = (
            jnp.dot(normed, w_dt[layer], preferred_element_type=jnp.float32)
            .astype(jnp.bfloat16)
            .reshape(seq_rows, draft, heads_here)
        )
        bc = (
            jnp.dot(normed, whole_bc[0][layer], preferred_element_type=jnp.float32)
            .astype(jnp.bfloat16)
            .reshape(seq_rows, draft, -1)
        )
        window_bc = jnp.concatenate([whole_bc[3][layer], bc], axis=1)
        bcc = convolve(
            window_bc.astype(jnp.float32), whole_bc[1][layer], whole_bc[2][layer], draft
        ).astype(jnp.bfloat16)
        kept_bc = keep_rows(window_bc, accepted, kernel - 1)
        bcc = lax.optimization_barrier(bcc).astype(jnp.float32)
        kept_bc = lax.dynamic_slice_in_dim(kept_bc, lax.axis_index("heads") * bc_here, bc_here, 2)
        states = bcc.shape[2] // 2
        bmat = bcc[..., :states]
        cmat = bcc[..., states:]
        window_x = jnp.concatenate([conv_x_state[layer], values], axis=1)
        xc = convolve(
            window_x.astype(jnp.float32), conv_x_w[layer], conv_x_b[layer], draft
        ).reshape(seq_rows, draft, heads_here, width)
        step = jax.nn.softplus(dt_raw.astype(jnp.float32) + dt_bias[layer])
        decay = jnp.exp(-step * decay_rate[layer])
        outputs, kept = recur_heads(
            decay, step, xc, bmat, cmat, skip_weight[layer], ssm_state[layer], accepted
        )
        saved_state.append(kept)
        saved_x.append(keep_rows(window_x, accepted, kernel - 1))
        saved_bc.append(kept_bc)
        gated = outputs * jax.nn.silu(gate_z)
        local_sq = jnp.sum(gated * gated, axis=(2, 3)).reshape(-1)
        u_rows = (
            (gated.reshape(seq_rows, draft, local_inner) * gate_gain[layer])
            .astype(jnp.bfloat16)
            .reshape(-1, local_inner)
        )
        return (u_rows, local_sq)

    part = embedding[draft_ids.reshape(-1)]
    stream = gather_directly(part, "heads", 1)
    where_cols = lax.axis_index("heads") * own_cols
    result = part
    for layer in range(LAYERS):
        u_rows, local_sq = mixer(layer, stream)
        term = jnp.dot(u_rows, out_w[layer], preferred_element_type=jnp.float32)
        total, ssq = lax.psum((term, local_sq), "heads")
        mix = total * rms_scale(ssq, inner)[:, None]
        if layer + 1 < LAYERS:
            stream = (stream.astype(jnp.float32) + mix).astype(jnp.bfloat16)
        else:
            own_stream = lax.dynamic_slice_in_dim(stream, where_cols, own_cols, 1)
            own_mix = lax.dynamic_slice_in_dim(mix, where_cols, own_cols, 1)
            result = (own_stream.astype(jnp.float32) + own_mix).astype(jnp.bfloat16)
    return (result, jnp.stack(saved_state), jnp.stack(saved_x), jnp.stack(saved_bc))


def solution(mesh):
    placed = (
        P("batch", None),
        P("batch"),
        P(None, "heads"),
        P(),
        P(None, None, "heads", None),
        P(None, None, "heads"),
        P(None, None, "heads"),
        P(None, "heads"),
        P(None, "heads"),
        P(None, "heads"),
        P(None, None, "heads"),
        P(None, "heads"),
        P(None, None, "heads"),
        P(None, "heads"),
        P(None, "heads"),
        P(None, "heads", None),
        P(None, "batch", "heads", None, None),
        P(None, "batch", None, "heads"),
        P(None, "batch", None, "heads"),
    )
    return jax.shard_map(
        local,
        mesh=mesh,
        in_specs=placed,
        out_specs=(
            P("batch", "heads"),
            P(None, "batch", "heads", None, None),
            P(None, "batch", None, "heads"),
            P(None, "batch", None, "heads"),
        ),
        check_vma=False,
    )
```

profile of v0, /device:TPU:2, one launch (start us, length us, event | category | flops | bytes accessed | tf_op | source)
XLA Modules:
  0.0 601.9 jit_solution(6505205176545360938)
XLA Ops:
  7.2 11.0 %copy.97 = bf16[50280,40]{1,0:T(8,128)(2,1)} copy(bf16[50280,40]{0,1:T(8,128)(2,1)} %param.21) | data formatting | bytes 8044800 | tf_op args[2]
  18.4 7.5 %gather_fusion = bf16[384,40]{1,0:T(8,128)(2,1)S(1)} fusion(bf16[50280,40]{1,0:T(8,128)(2,1)} %copy.97, s32[1024]{0:T(1024)S(1)} %pad_clamp_fusion), kind=kCustom, calls=%fused_computation | custom fusion | bytes 62976 | tf_op jit(solution)/shard_map/gather | solution.py:162
  26.0 1.4 broadcast_in_dim.263
  27.5 12.2 %all-to-all-start = ((bf16[64,384,40]{1,2,0:T(8,128)(2,1)}), bf16[64,384,40]{1,2,0:T(8,128)(2,1)S(1)}, u32[]{:S(2)}, u32[]{:S(2)}) async-start(bf16[64,384,40]{1,2,0:T(8,128)(2,1)} %broadcast_in_dim.263), calls=%async_computation | async-start | bytes 3932160 | tf_op jit(solution)/shard_map/all_to_all | solution.py:32
  45.7 43.7 %all-to-all-done = bf16[64,384,40]{1,2,0:T(8,128)(2,1)S(1)} async-done(((bf16[64,384,40]{1,2,0:T(8,128)(2,1)}), bf16[64,384,40]{1,2,0:T(8,128)(2,1)S(1)}, u32[]{:S(2)}, u32[]{:S(2)}) %all-to-all-start) | async-done | bytes 1966112 | tf_op jit(solution)/shard_map/all_to_all | solution.py:32
  90.5 1.3 copy-done.3
  93.0 2.0 convolution_reduce_fusion.1
  98.5 26.6 %all-gather.3.cloned.1.call-done = bf16[64,4,5418]{2,1,0:T(4,128)(2,1)} async-done(((bf16[1,4,5418]{2,1,0:T(4,128)(2,1)}), bf16[64,4,5418]{2,1,0:T(4,128)(2,1)}) %all-gather.3.cloned.1.call-update) | async-done | bytes 2774032 | tf_op jit(solution)/shard_map/all_gather | solution.py:14
  125.0 5.5 reshape.2596
  130.6 3.6 split.17
  134.3 4.4 copy.128
  138.8 2.7 fusion.10
  145.8 4.1 multiply_add_fusion.8
  150.6 1.7 multiply_reduce_fusion.13
  154.1 3.7 multiply_reduce_fusion.9
  160.3 2.5 fusion.27
  164.1 2.2 convert_element_type.337
  166.3 5.6 copy.109
  172.0 1.4 fusion.103
  174.7 127.0 %psum.29 = f32[384]{0:T(512)S(1)} all-reduce(f32[384]{0:T(512)S(1)} %reshape.2572), channel_id=1, replica_groups=mesh['batch'=4,'heads'=64] {'heads'}, use_global_device_ids=true, to_apply=%region_11.12 | all-reduce | flops 384 | bytes 3072 | tf_op jit(solution)/shard_map/psum | solution.py:169
  301.7 1.4 fusion.119
  303.1 9.0 %select_select_fusion.1 = f32[1,48,1,64,128]{4,3,2,1,0:T(8,128)} fusion(f32[2,48,1,64,128]{4,3,2,1,0:T(8,128)S(1)} %copy-done.1, f32[48,128]{1,0:T(8,128)} %bitcast.581, f32[48,64]{1,0:T(8,128)} %copy-done.34, f32[48,128]{1,0:T(8,128)} %bitcast.579, f32[48,64]{1,0:T(8,128)} %copy-done.35, f32[48,128]{1,0:T(8,128)S(1)} %bitcast.577, f32[48,64]{1,0:T(8,128)} %copy-done.33, ...), kind=kLoop, calls=%fused_computation.15 | loop fusion | flops 12582912 | bytes 3442560 | tf_op jit(solution)/shard_map/vmap(jit(_where))/select_n | solution.py:72
  312.1 43.3 %all-reduce.3.cloned.1.call-done = f32[384,2560]{1,0:T(8,128)} async-done(((f32[384,2560]{1,0:T(8,128)}), f32[384,2560]{1,0:T(8,128)}) %all-reduce.3.cloned.1.call-update) | async-done | bytes 3932176 | tf_op jit(solution)/shard_map/psum | solution.py:169
  355.4 4.2 fusion
  360.4 1.3 copy-done.91
  361.6 1.4 convolution_convert_fusion
  363.0 1.3 convolution_reduce_fusion
  364.3 1.7 reshape.2574
  366.1 2.1 fusion.115
  369.7 1.4 fusion.127
  371.9 1.8 fusion.113
  375.5 2.2 multiply_convert_fusion.1
  380.8 4.1 multiply_add_fusion.2
  385.6 1.7 multiply_reduce_fusion.5
  389.2 3.7 multiply_reduce_fusion.1
  394.7 1.3 constant_dynamic-update-slice_fusion.24
  396.8 2.6 fusion.25
  399.3 2.2 dynamic-slice_select_fusion.6
  401.5 1.5 copy.123
  403.0 2.1 dynamic-slice_select_fusion
  405.2 1.4 copy.124
  406.6 1.7 fusion.71
  409.2 128.1 %psum.31 = f32[384]{0:T(512)S(1)} all-reduce(f32[384]{0:T(512)S(1)} %reshape.2577), channel_id=1, replica_groups=mesh['batch'=4,'heads'=64] {'heads'}, use_global_device_ids=true, to_apply=%region_23.24 | all-reduce | flops 384 | bytes 3072 | tf_op jit(solution)/shard_map/psum | solution.py:169
  537.3 1.3 pad_maximum_fusion.6
  539.4 1.4 pad_maximum_fusion.5
  540.8 8.3 %select_select_fusion = f32[1,48,1,64,128]{4,3,2,1,0:T(8,128)S(1)} fusion(f32[2,48,1,64,128]{4,3,2,1,0:T(8,128)S(1)} %copy-done.1, f32[48,128]{1,0:T(8,128)} %bitcast.567, f32[48,64]{1,0:T(8,128)} %copy-done.40, f32[48,128]{1,0:T(8,128)} %bitcast.565, f32[48,64]{1,0:T(8,128)} %copy-done.42, f32[48,128]{1,0:T(8,128)S(1)} %bitcast.563, ...), kind=kLoop, calls=%fused_computation.14 | loop fusion | flops 12582912 | bytes 3442560 | tf_op jit(solution)/shard_map/vmap(jit(_where))/select_n | solution.py:72
  549.1 1.9 pad_maximum_fusion
  551.0 42.4 %all-reduce.5.cloned.1.call-done = f32[384,2560]{1,0:T(8,128)} async-done(((f32[384,2560]{1,0:T(8,128)}), f32[384,2560]{1,0:T(8,128)}) %all-reduce.5.cloned.1.call-update) | async-done | bytes 3932176 | tf_op jit(solution)/shard_map/psum | solution.py:169
  (282 shorter events, 39.9 us)
Async XLA Ops:
  7.2 11.0 %copy-start.78 = (s32[48,8]{0,1:T(8,128)S(1)}, s32[48,8]{0,1:T(8,128)}, u32[]{:S(2)}) copy-start(s32[48,8]{0,1:T(8,128)} %param.19) | copy-start | bytes 4612
  27.4 12.4 %copy-start.56 = (bf16[2,48,3,4]{1,3,2,0:T(4,128)(2,1)S(1)}, bf16[2,48,3,4]{1,3,2,0:T(4,128)(2,1)}, u32[]{:S(2)}) copy-start(bf16[2,48,3,4]{1,3,2,0:T(4,128)(2,1)} %param.37) | copy-start | bytes 6916
  27.4 12.8 %copy-start.92 = (bf16[2,4]{1,0:T(2,128)(2,1)S(1)}, bf16[2,4]{1,0:T(2,128)(2,1)}, u32[]{:S(2)}) copy-start(bf16[2,4]{1,0:T(2,128)(2,1)} %param.32) | copy-start | bytes 52
  27.4 12.9 %copy-start.82 = (bf16[2,4,4]{2,1,0:T(4,128)(2,1)S(1)}, bf16[2,4,4]{2,1,0:T(4,128)(2,1)}, u32[]{:S(2)}) copy-start(bf16[2,4,4]{2,1,0:T(4,128)(2,1)} %param.31) | copy-start | bytes 196
  27.4 13.0 %copy-start.48 = (bf16[2,2560,4]{1,2,0:T(4,128)(2,1)S(1)}, bf16[2,2560,4]{1,2,0:T(4,128)(2,1)}, u32[]{:S(2)}) copy-start(bf16[2,2560,4]{1,2,0:T(4,128)(2,1)} %param.25) | copy-start | bytes 122884
  27.4 13.9 %copy-start.49 = (f32[2,2560]{1,0:T(2,128)S(1)}, f32[2,2560]{1,0:T(2,128)}, u32[]{:S(2)}) copy-start(f32[2,2560]{1,0:T(2,128)} %param.22) | copy-start | bytes 61444
  27.5 14.7 %copy-start.83 = (f32[2,1]{0,1:T(1,128)S(1)}, f32[2,1]{0,1:T(1,128)}, u32[]{:S(2)}) copy-start(f32[2,1]{0,1:T(1,128)} %param.26) | copy-start | bytes 28
  27.5 15.3 %copy-start.84 = (f32[2,1]{0,1:T(1,128)S(1)}, f32[2,1]{0,1:T(1,128)}, u32[]{:S(2)}) copy-start(f32[2,1]{0,1:T(1,128)} %param.27) | copy-start | bytes 28
  27.5 15.9 %copy-start.85 = (f32[2,1]{0,1:T(1,128)S(1)}, f32[2,1]{0,1:T(1,128)}, u32[]{:S(2)}) copy-start(f32[2,1]{0,1:T(1,128)} %param.28) | copy-start | bytes 28
  27.5 16.4 %copy-start.86 = (bf16[2,64]{1,0:T(2,128)(2,1)S(1)}, bf16[2,64]{1,0:T(2,128)(2,1)}, u32[]{:S(2)}) copy-start(bf16[2,64]{1,0:T(2,128)(2,1)} %param.30) | copy-start | bytes 772
  27.5 17.0 %copy-start.88 = (f32[2,64]{1,0:T(2,128)S(1)}, f32[2,64]{1,0:T(2,128)}, u32[]{:S(2)}) copy-start(f32[2,64]{1,0:T(2,128)} %param.33) | copy-start | bytes 1540
  27.5 17.6 %copy-start.81 = (bf16[2,4,64]{2,1,0:T(4,128)(2,1)S(1)}, bf16[2,4,64]{2,1,0:T(4,128)(2,1)}, u32[]{:S(2)}) copy-start(bf16[2,4,64]{2,1,0:T(4,128)(2,1)} %param.29) | copy-start | bytes 3076
  27.5 17.6 %copy-start.47 = (bf16[2,48,3,64]{3,1,2,0:T(8,128)(2,1)S(1)}, bf16[2,48,3,64]{3,1,2,0:T(8,128)(2,1)}, u32[]{:S(2)}) copy-start(bf16[2,48,3,64]{3,1,2,0:T(8,128)(2,1)} %param.36) | copy-start | bytes 110596
  27.5 61.9 %all-to-all-start = ((bf16[64,384,40]{1,2,0:T(8,128)(2,1)}), bf16[64,384,40]{1,2,0:T(8,128)(2,1)S(1)}, u32[]{:S(2)}, u32[]{:S(2)}) async-start(bf16[64,384,40]{1,2,0:T(8,128)(2,1)} %broadcast_in_dim.263), calls=%async_computation | async-start | bytes 3932160 | tf_op jit(solution)/shard_map/all_to_all | solution.py:32
  39.8 85.3 %all-gather.3.cloned.1.call-start = ((), (), s32[]{:S(2)}) async-start(), calls=%async_computation.3 | async-start | bytes 2862080 | tf_op jit(solution)/shard_map/all_gather | solution.py:14
  41.2 314.3 %all-reduce.3.cloned.1.call-start = ((), (), s32[]{:S(2)}) async-start(), calls=%async_computation.1 | async-start | bytes 7864320 | tf_op jit(solution)/shard_map/psum | solution.py:169
  92.9 67.3 %copy-start.9 = (bf16[48,8,1,1,64]{4,3,1,0,2:T(2,128)(2,1)}, bf16[48,8,1,1,64]{4,3,1,0,2:T(2,128)(2,1)S(1)}, u32[]{:S(2)}) copy-start(bf16[48,8,1,1,64]{4,3,1,0,2:T(2,128)(2,1)S(1)} %get-tuple-element.155) | copy-start | bytes 147460
  97.6 47.0 %copy-start.62 = (f32[48]{0:T(128)}, f32[48]{0:T(128)S(1)}, u32[]{:S(2)}) copy-start(f32[48]{0:T(128)S(1)} %get-tuple-element.57) | copy-start | bytes 580
  97.6 53.0 %copy-start.54 = (f32[48]{0:T(128)}, f32[48]{0:T(128)S(1)}, u32[]{:S(2)}) copy-start(f32[48]{0:T(128)S(1)} %get-tuple-element.58) | copy-start | bytes 580
  98.5 46.2 %copy-start.36 = (f32[48,64]{1,0:T(8,128)}, f32[48,64]{1,0:T(8,128)S(1)}, u32[]{:S(2)}) copy-start(f32[48,64]{1,0:T(8,128)S(1)} %get-tuple-element.176) | copy-start | bytes 36868
  98.5 55.6 %copy-start.33 = (f32[48,64]{1,0:T(8,128)}, f32[48,64]{1,0:T(8,128)S(1)}, u32[]{:S(2)}) copy-start(f32[48,64]{1,0:T(8,128)S(1)} %get-tuple-element.173) | copy-start | bytes 36868
  98.5 55.6 %copy-start.34 = (f32[48,64]{1,0:T(8,128)}, f32[48,64]{1,0:T(8,128)S(1)}, u32[]{:S(2)}) copy-start(f32[48,64]{1,0:T(8,128)S(1)} %get-tuple-element.174) | copy-start | bytes 36868
  98.5 55.6 %copy-start.35 = (f32[48,64]{1,0:T(8,128)}, f32[48,64]{1,0:T(8,128)S(1)}, u32[]{:S(2)}) copy-start(f32[48,64]{1,0:T(8,128)S(1)} %get-tuple-element.175) | copy-start | bytes 36868
  144.6 9.5 %copy-start.27 = (f32[48,1,128]{2,1,0:T(1,128)}, f32[48,1,128]{2,1,0:T(1,128)S(1)}, u32[]{:S(2)}) copy-start(f32[48,1,128]{2,1,0:T(1,128)S(1)} %get-tuple-element.161) | copy-start | bytes 73732
  144.6 9.5 %copy-start.28 = (f32[48,1,128]{2,1,0:T(1,128)}, f32[48,1,128]{2,1,0:T(1,128)S(1)}, u32[]{:S(2)}) copy-start(f32[48,1,128]{2,1,0:T(1,128)S(1)} %get-tuple-element.162) | copy-start | bytes 73732
  152.2 7.9 %copy-start.80 = (f32[64]{0:T(128)S(1)}, f32[64]{0:T(128)}, u32[]{:S(2)}) copy-start(f32[64]{0:T(128)} %get-tuple-element.208) | copy-start | bytes 772
  152.3 8.0 %copy-start.16 = (bf16[2,64,2560]{2,1,0:T(8,128)(2,1)S(1)}, bf16[2,64,2560]{2,1,0:T(8,128)(2,1)}, u32[]{:S(2)}) copy-start(bf16[2,64,2560]{2,1,0:T(8,128)(2,1)} %param.34) | copy-start | bytes 1966084
  162.8 430.5 %all-reduce.5.cloned.1.call-start = ((), (), s32[]{:S(2)}) async-start(), calls=%async_computation.2 | async-start | bytes 7864320 | tf_op jit(solution)/shard_map/psum | solution.py:169
  166.3 136.8 %copy-start.1 = (f32[2,48,1,64,128]{4,3,2,1,0:T(8,128)S(1)}, f32[2,48,1,64,128]{4,3,2,1,0:T(8,128)}, u32[]{:S(2)}) copy-start(f32[2,48,1,64,128]{4,3,2,1,0:T(8,128)} %param.35) | copy-start | bytes 9437188
  312.1 47.5 %copy-start.51 = (f32[2560]{0:T(1024)S(1)}, f32[2560]{0:T(1024)}, u32[]{:S(2)}) copy-start(f32[2560]{0:T(1024)} %get-tuple-element.70) | copy-start | bytes 30724
  377.9 7.0 %copy-start.23 = (f32[48,1,128]{2,1,0:T(1,128)}, f32[48,1,128]{2,1,0:T(1,128)S(1)}, u32[]{:S(2)}) copy-start(f32[48,1,128]{2,1,0:T(1,128)S(1)} %get-tuple-element.137) | copy-start | bytes 73732
  377.9 7.0 %copy-start.24 = (f32[48,1,128]{2,1,0:T(1,128)}, f32[48,1,128]{2,1,0:T(1,128)S(1)}, u32[]{:S(2)}) copy-start(f32[48,1,128]{2,1,0:T(1,128)S(1)} %get-tuple-element.141) | copy-start | bytes 73732
  377.9 7.0 %copy-start.25 = (f32[48,1,128]{2,1,0:T(1,128)}, f32[48,1,128]{2,1,0:T(1,128)S(1)}, u32[]{:S(2)}) copy-start(f32[48,1,128]{2,1,0:T(1,128)S(1)} %get-tuple-element.143) | copy-start | bytes 73732
  377.9 7.0 %copy-start.26 = (f32[48,1,128]{2,1,0:T(1,128)}, f32[48,1,128]{2,1,0:T(1,128)S(1)}, u32[]{:S(2)}) copy-start(f32[48,1,128]{2,1,0:T(1,128)S(1)} %get-tuple-element.144) | copy-start | bytes 73732
  377.9 11.2 %copy-start.21 = (f32[48,1,128]{2,1,0:T(1,128)}, f32[48,1,128]{2,1,0:T(1,128)S(1)}, u32[]{:S(2)}) copy-start(f32[48,1,128]{2,1,0:T(1,128)S(1)} %get-tuple-element.134) | copy-start | bytes 73732
  377.9 11.2 %copy-start.22 = (f32[48,1,128]{2,1,0:T(1,128)}, f32[48,1,128]{2,1,0:T(1,128)S(1)}, u32[]{:S(2)}) copy-start(f32[48,1,128]{2,1,0:T(1,128)S(1)} %get-tuple-element.135) | copy-start | bytes 73732
  379.2 10.0 %copy-start.73 = (f32[48]{0:T(128)}, f32[48]{0:T(128)S(1)}, u32[]{:S(2)}) copy-start(f32[48]{0:T(128)S(1)} %get-tuple-element.237) | copy-start | bytes 580
  379.2 10.0 %copy-start.74 = (f32[48]{0:T(128)}, f32[48]{0:T(128)S(1)}, u32[]{:S(2)}) copy-start(f32[48]{0:T(128)S(1)} %get-tuple-element.238) | copy-start | bytes 580
  379.2 10.0 %copy-start.75 = (f32[48]{0:T(128)}, f32[48]{0:T(128)S(1)}, u32[]{:S(2)}) copy-start(f32[48]{0:T(128)S(1)} %get-tuple-element.239) | copy-start | bytes 580
  380.0 9.2 %copy-start.40 = (f32[48,64]{1,0:T(8,128)}, f32[48,64]{1,0:T(8,128)S(1)}, u32[]{:S(2)}) copy-start(f32[48,64]{1,0:T(8,128)S(1)} %bitcast_multiply_fusion.2) | copy-start | bytes 36868
  380.2 9.0 %copy-start.41 = (f32[48,64]{1,0:T(8,128)}, f32[48,64]{1,0:T(8,128)S(1)}, u32[]{:S(2)}) copy-start(f32[48,64]{1,0:T(8,128)S(1)} %get-tuple-element.146) | copy-start | bytes 36868
  380.2 9.0 %copy-start.42 = (f32[48,64]{1,0:T(8,128)}, f32[48,64]{1,0:T(8,128)S(1)}, u32[]{:S(2)}) copy-start(f32[48,64]{1,0:T(8,128)S(1)} %get-tuple-element.147) | copy-start | bytes 36868
  387.3 9.4 %copy-start.10 = (bf16[48,8,1,1,64]{4,3,1,0,2:T(2,128)(2,1)S(1)}, bf16[48,8,1,1,64]{4,3,1,0,2:T(2,128)(2,1)}, u32[]{:S(2)}) copy-start(bf16[48,8,1,1,64]{4,3,1,0,2:T(2,128)(2,1)} %get-tuple-element.128) | copy-start | bytes 147460
  387.3 9.4 %copy-start.79 = (f32[64]{0:T(128)S(1)}, f32[64]{0:T(128)}, u32[]{:S(2)}) copy-start(f32[64]{0:T(128)} %get-tuple-element.207) | copy-start | bytes 772
  387.3 9.4 %copy-start.17 = (bf16[2,64,2560]{2,1,0:T(8,128)(2,1)S(1)}, bf16[2,64,2560]{2,1,0:T(8,128)(2,1)}, u32[]{:S(2)}) copy-start(bf16[2,64,2560]{2,1,0:T(8,128)(2,1)} %param.34) | copy-start | bytes 1966084
  399.3 139.2 %copy-start.18 = (bf16[48,3,64]{2,0,1:T(8,128)(2,1)S(1)}, bf16[48,3,64]{2,0,1:T(8,128)(2,1)}, u32[]{:S(2)}) copy-start(bf16[48,3,64]{2,0,1:T(8,128)(2,1)} %get-tuple-element.181) | copy-start | bytes 55300
  399.3 139.2 %copy-start.6 = (bf16[48,8,1,1,64]{4,0,1,3,2:T(8,128)(2,1)S(1)}, bf16[48,8,1,1,64]{4,0,1,3,2:T(8,128)(2,1)}, u32[]{:S(2)}) copy-start(bf16[48,8,1,1,64]{4,0,1,3,2:T(8,128)(2,1)} %copy-done.5) | copy-start | bytes 147460
  540.8 8.3 %copy-start.4 = (f32[1,48,1,64,128]{4,3,2,1,0:T(8,128)S(1)}, f32[1,48,1,64,128]{4,3,2,1,0:T(8,128)}, u32[]{:S(2)}) copy-start(f32[1,48,1,64,128]{4,3,2,1,0:T(8,128)} %select_select_fusion.1) | copy-start | bytes 4718596
  (50 other events, 168.0 us)
Sparse Core Ops, SparseCore 0:
  43.9 81.1 all-gather.2
  163.0 192.4 all-reduce.2
  399.5 193.8 all-reduce.4
where the time goes:
time: 604 us; the launch traced here: 602 us
  blocking collectives  255 us (42%)
  waiting for transfers between devices  156 us (26%)
  other arithmetic  84.4 us (14%)
  local copies, waits for them, and re-layouts  64.7 us (11%)
  between operations  15.2 us (3%)
  matrix products  13.8 us (2%)
  starting transfers between devices  12.6 us (2%)
    psum x2, blocking collectives, local(): total, ssq = lax.psum((term, local_sq), 'heads')  255 us
    psum x2, waiting for transfers between devices, local(): total, ssq = lax.psum((term, local_sq), 'heads')  85.7 us
    all_to_all x1, waiting for transfers between devices, sent_to_all(): lax.all_to_all(jnp.broadcast_to(value[None], (count, *value.shape)), axis...  43.7 us
    all_gather x1, waiting for transfers between devices, turned_gather(): filled = lax.all_gather(both, axis, axis=0, tiled=True)  26.6 us
    unnamed x193, local copies, waits for them, and re-layouts  23.4 us
    select_n x2, other arithmetic, recur(): kept = jnp.where((accepted == t + 1)[:, None, None], state, kept)  17.3 us
    all_to_all x1, starting transfers between devices, sent_to_all(): lax.all_to_all(jnp.broadcast_to(value[None], (count, *value.shape)), axis...  12.2 us
  transfers between devices with their start and end apart: 4, of which 4 were waited for; matrix products, arithmetic and copies ran while one was open for 10% of the time, Pallas kernels for 0%

commit v1 on v0

--- a/solution.py
+++ b/solution.py
@@ -11,7 +11,9 @@
     turned = [jnp.moveaxis(a, dim, 0) for a, dim in zip(arrays, dims)]
     widths = [t[0].size for t in turned]
     both = jnp.concatenate([t.reshape(-1, w) for t, w in zip(turned, widths)], axis=1)
-    filled = lax.all_gather(both, axis, axis=0, tiled=True)
+    filled = jnp.concatenate(
+        lax.all_to_all(jnp.stack([both] * lax.axis_size(axis)), axis, 0, 0), axis=0
+    )
     blocks = jnp.split(filled, [sum(widths[:k]) for k in range(1, len(widths))], axis=1)
     return tuple(
         (

time: 604 us -> 642 us (1.063)
  waiting for transfers between devices: 156 us -> 187 us
    all_to_all x0 -> x1, waiting for transfers between devices: none -> 52 us  [turned_gather(): lax.all_to_all(jnp.stack([both] * lax.axis_size(axis)), axis, 0, 0)]
    all_gather x1 -> x0, waiting for transfers between devices: 26.6 us -> none  [turned_gather(): filled = lax.all_gather(both, axis, axis=0, tiled=True)]
    all_to_all x0 -> x1, starting transfers between devices: none -> 6.49 us  [turned_gather(): lax.all_to_all(jnp.stack([both] * lax.axis_size(axis)), axis, 0, 0)]
    unnamed x193 -> x192, local copies, waits for them, and re-layouts: 23.4 us -> 17.9 us
  transfers between devices with their start and end apart: 4 -> 4, of which waited for: 4 -> 4; matrix products, arithmetic and copies ran while one was open for 10% -> 9% of each run, Pallas kernels for 0% -> 0%
where the time goes in v1:
time: 642 us; the launch traced here: 640 us
  blocking collectives  254 us (40%)
  waiting for transfers between devices  187 us (29%)
  other arithmetic  84.4 us (13%)
  local copies, waits for them, and re-layouts  66.4 us (10%)
  starting transfers between devices  19 us (3%)
  between operations  15.5 us (2%)
  matrix products  13.9 us (2%)
    psum x2, blocking collectives, local(): total, ssq = lax.psum((term, local_sq), 'heads')  254 us
    psum x2, waiting for transfers between devices, local(): total, ssq = lax.psum((term, local_sq), 'heads')  87 us
    all_to_all x1, waiting for transfers between devices, turned_gather(): lax.all_to_all(jnp.stack([both] * lax.axis_size(axis)), axis, 0, 0)  52 us
    all_to_all x1, waiting for transfers between devices, sent_to_all(): lax.all_to_all(jnp.broadcast_to(value[None], (count, *value.shape)), axis...  47.5 us
    unnamed x192, local copies, waits for them, and re-layouts  17.9 us
    select_n x2, other arithmetic, recur(): kept = jnp.where((accepted == t + 1)[:, None, None], state, kept)  17.3 us
  transfers between devices with their start and end apart: 4, of which 4 were waited for; matrix products, arithmetic and copies ran while one was open for 9% of the time, Pallas kernels for 0%

profile of v1, /device:TPU:2, one launch (start us, length us, event | category | flops | bytes accessed | tf_op | source)
XLA Modules:
  0.0 639.5 jit_solution(16953221342350199314)
XLA Ops:
  7.2 11.0 %copy.97 = bf16[50280,40]{1,0:T(8,128)(2,1)} copy(bf16[50280,40]{0,1:T(8,128)(2,1)} %param.21) | data formatting | bytes 8044800 | tf_op args[2]
  18.4 7.5 %gather_fusion = bf16[384,40]{1,0:T(8,128)(2,1)S(1)} fusion(bf16[50280,40]{1,0:T(8,128)(2,1)} %copy.97, s32[1024]{0:T(1024)S(1)} %pad_clamp_fusion), kind=kCustom, calls=%fused_computation | custom fusion | bytes 62976 | tf_op jit(solution)/shard_map/gather | solution.py:164
  26.0 1.4 broadcast_in_dim.263
  27.4 12.3 %all-to-all-start = ((bf16[64,384,40]{1,2,0:T(8,128)(2,1)}), bf16[64,384,40]{1,2,0:T(8,128)(2,1)S(1)}, u32[]{:S(2)}, u32[]{:S(2)}) async-start(bf16[64,384,40]{1,2,0:T(8,128)(2,1)} %broadcast_in_dim.263), calls=%async_computation | async-start | bytes 3932160 | tf_op jit(solution)/shard_map/all_to_all | solution.py:34
  40.4 47.5 %all-to-all-done = bf16[64,384,40]{1,2,0:T(8,128)(2,1)S(1)} async-done(((bf16[64,384,40]{1,2,0:T(8,128)(2,1)}), bf16[64,384,40]{1,2,0:T(8,128)(2,1)S(1)}, u32[]{:S(2)}, u32[]{:S(2)}) %all-to-all-start) | async-done | bytes 1966112 | tf_op jit(solution)/shard_map/all_to_all | solution.py:34
  87.8 2.3 stack.56
  90.2 6.5 %all-to-all-start.1 = ((bf16[64,4,5418]{2,1,0:T(4,128)(2,1)}), bf16[64,4,5418]{2,1,0:T(4,128)(2,1)}, u32[]{:S(2)}, u32[]{:S(2)}) async-start(bf16[64,4,5418]{2,1,0:T(4,128)(2,1)} %stack.56), calls=%async_computation.1 | async-start | bytes 5636096 | tf_op jit(solution)/shard_map/all_to_all | solution.py:15
  104.8 2.0 convolution_reduce_fusion.1
  110.3 52.0 %all-to-all-done.1 = bf16[64,4,5418]{2,1,0:T(4,128)(2,1)} async-done(((bf16[64,4,5418]{2,1,0:T(4,128)(2,1)}), bf16[64,4,5418]{2,1,0:T(4,128)(2,1)}, u32[]{:S(2)}, u32[]{:S(2)}) %all-to-all-start.1) | async-done | bytes 2774048 | tf_op jit(solution)/shard_map/all_to_all | solution.py:15
  162.3 5.5 reshape.2573
  167.8 3.6 split.17
  171.6 4.4 copy.128
  176.0 2.7 fusion.10
  183.0 4.1 multiply_add_fusion.8
  187.8 1.7 multiply_reduce_fusion.13
  191.4 3.7 multiply_reduce_fusion.9
  197.5 2.6 fusion.27
  201.4 2.2 convert_element_type.337
  203.6 5.6 copy.109
  209.2 1.4 fusion.103
  212.0 125.7 %psum.29 = f32[384]{0:T(512)S(1)} all-reduce(f32[384]{0:T(512)S(1)} %reshape.2578), channel_id=1, replica_groups=mesh['batch'=4,'heads'=64] {'heads'}, use_global_device_ids=true, to_apply=%region_11.12 | all-reduce | flops 384 | bytes 3072 | tf_op jit(solution)/shard_map/psum | solution.py:171
  337.7 1.4 fusion.119
  339.1 9.0 %select_select_fusion.1 = f32[1,48,1,64,128]{4,3,2,1,0:T(8,128)} fusion(f32[2,48,1,64,128]{4,3,2,1,0:T(8,128)S(1)} %copy-done.1, f32[48,128]{1,0:T(8,128)} %bitcast.580, f32[48,64]{1,0:T(8,128)} %copy-done.34, f32[48,128]{1,0:T(8,128)} %bitcast.578, f32[48,64]{1,0:T(8,128)} %copy-done.35, f32[48,128]{1,0:T(8,128)S(1)} %bitcast.576, f32[48,64]{1,0:T(8,128)} %copy-done.33, ...), kind=kLoop, calls=%fused_computation.15 | loop fusion | flops 12582912 | bytes 3442560 | tf_op jit(solution)/shard_map/vmap(jit(_where))/select_n | solution.py:74
  348.1 44.6 %all-reduce.3.cloned.1.call-done = f32[384,2560]{1,0:T(8,128)} async-done(((f32[384,2560]{1,0:T(8,128)}), f32[384,2560]{1,0:T(8,128)}) %all-reduce.3.cloned.1.call-update) | async-done | bytes 3932176 | tf_op jit(solution)/shard_map/psum | solution.py:171
  392.7 4.2 fusion
  399.0 1.4 convolution_convert_fusion
  400.4 1.3 convolution_reduce_fusion
  401.7 1.7 reshape.2580
  403.4 2.1 fusion.115
  407.0 1.4 fusion.127
  409.2 1.8 fusion.113
  412.8 2.2 multiply_convert_fusion.1
  418.1 4.1 multiply_add_fusion.2
  422.9 1.7 multiply_reduce_fusion.5
  426.5 3.7 multiply_reduce_fusion.1
  432.0 1.3 constant_dynamic-update-slice_fusion.24
  434.1 2.5 fusion.25
  436.7 2.2 dynamic-slice_select_fusion.6
  438.9 1.5 copy.123
  440.3 2.1 dynamic-slice_select_fusion
  442.5 1.4 copy.124
  443.9 1.7 fusion.71
  446.5 128.1 %psum.31 = f32[384]{0:T(512)S(1)} all-reduce(f32[384]{0:T(512)S(1)} %reshape.2583), channel_id=1, replica_groups=mesh['batch'=4,'heads'=64] {'heads'}, use_global_device_ids=true, to_apply=%region_23.24 | all-reduce | flops 384 | bytes 3072 | tf_op jit(solution)/shard_map/psum | solution.py:171
  574.6 1.3 pad_maximum_fusion.6
  576.7 1.4 pad_maximum_fusion.5
  578.1 8.3 %select_select_fusion = f32[1,48,1,64,128]{4,3,2,1,0:T(8,128)S(1)} fusion(f32[2,48,1,64,128]{4,3,2,1,0:T(8,128)S(1)} %copy-done.1, f32[48,128]{1,0:T(8,128)} %bitcast.566, f32[48,64]{1,0:T(8,128)} %copy-done.40, f32[48,128]{1,0:T(8,128)} %bitcast.564, f32[48,64]{1,0:T(8,128)} %copy-done.42, f32[48,128]{1,0:T(8,128)S(1)} %bitcast.562, ...), kind=kLoop, calls=%fused_computation.14 | loop fusion | flops 12582912 | bytes 3442560 | tf_op jit(solution)/shard_map/vmap(jit(_where))/select_n | solution.py:74
  586.4 1.9 pad_maximum_fusion
  588.3 42.4 %all-reduce.5.cloned.1.call-done = f32[384,2560]{1,0:T(8,128)} async-done(((f32[384,2560]{1,0:T(8,128)}), f32[384,2560]{1,0:T(8,128)}) %all-reduce.5.cloned.1.call-update) | async-done | bytes 3932176 | tf_op jit(solution)/shard_map/psum | solution.py:171
  (282 shorter events, 41.8 us)
Async XLA Ops:
  7.2 11.0 %copy-start.78 = (s32[48,8]{0,1:T(8,128)S(1)}, s32[48,8]{0,1:T(8,128)}, u32[]{:S(2)}) copy-start(s32[48,8]{0,1:T(8,128)} %param.19) | copy-start | bytes 4612
  27.4 12.3 %copy-start.56 = (bf16[2,48,3,4]{1,3,2,0:T(4,128)(2,1)S(1)}, bf16[2,48,3,4]{1,3,2,0:T(4,128)(2,1)}, u32[]{:S(2)}) copy-start(bf16[2,48,3,4]{1,3,2,0:T(4,128)(2,1)} %param.37) | copy-start | bytes 6916
  27.4 12.6 %copy-start.92 = (bf16[2,4]{1,0:T(2,128)(2,1)S(1)}, bf16[2,4]{1,0:T(2,128)(2,1)}, u32[]{:S(2)}) copy-start(bf16[2,4]{1,0:T(2,128)(2,1)} %param.32) | copy-start | bytes 52
  27.4 12.7 %copy-start.82 = (bf16[2,4,4]{2,1,0:T(4,128)(2,1)S(1)}, bf16[2,4,4]{2,1,0:T(4,128)(2,1)}, u32[]{:S(2)}) copy-start(bf16[2,4,4]{2,1,0:T(4,128)(2,1)} %param.31) | copy-start | bytes 196
  27.4 12.8 %copy-start.48 = (bf16[2,2560,4]{1,2,0:T(4,128)(2,1)S(1)}, bf16[2,2560,4]{1,2,0:T(4,128)(2,1)}, u32[]{:S(2)}) copy-start(bf16[2,2560,4]{1,2,0:T(4,128)(2,1)} %param.25) | copy-start | bytes 122884
  27.4 60.4 %all-to-all-start = ((bf16[64,384,40]{1,2,0:T(8,128)(2,1)}), bf16[64,384,40]{1,2,0:T(8,128)(2,1)S(1)}, u32[]{:S(2)}, u32[]{:S(2)}) async-start(bf16[64,384,40]{1,2,0:T(8,128)(2,1)} %broadcast_in_dim.263), calls=%async_computation | async-start | bytes 3932160 | tf_op jit(solution)/shard_map/all_to_all | solution.py:34
  90.1 6.8 %copy-start.49 = (f32[2,2560]{1,0:T(2,128)S(1)}, f32[2,2560]{1,0:T(2,128)}, u32[]{:S(2)}) copy-start(f32[2,2560]{1,0:T(2,128)} %param.22) | copy-start | bytes 61444
  90.1 7.5 %copy-start.83 = (f32[2,1]{0,1:T(1,128)S(1)}, f32[2,1]{0,1:T(1,128)}, u32[]{:S(2)}) copy-start(f32[2,1]{0,1:T(1,128)} %param.26) | copy-start | bytes 28
  90.1 8.1 %copy-start.84 = (f32[2,1]{0,1:T(1,128)S(1)}, f32[2,1]{0,1:T(1,128)}, u32[]{:S(2)}) copy-start(f32[2,1]{0,1:T(1,128)} %param.27) | copy-start | bytes 28
  90.1 8.7 %copy-start.85 = (f32[2,1]{0,1:T(1,128)S(1)}, f32[2,1]{0,1:T(1,128)}, u32[]{:S(2)}) copy-start(f32[2,1]{0,1:T(1,128)} %param.28) | copy-start | bytes 28
  90.1 9.3 %copy-start.86 = (bf16[2,64]{1,0:T(2,128)(2,1)S(1)}, bf16[2,64]{1,0:T(2,128)(2,1)}, u32[]{:S(2)}) copy-start(bf16[2,64]{1,0:T(2,128)(2,1)} %param.30) | copy-start | bytes 772
  90.1 9.9 %copy-start.88 = (f32[2,64]{1,0:T(2,128)S(1)}, f32[2,64]{1,0:T(2,128)}, u32[]{:S(2)}) copy-start(f32[2,64]{1,0:T(2,128)} %param.33) | copy-start | bytes 1540
  90.2 10.5 %copy-start.81 = (bf16[2,4,64]{2,1,0:T(4,128)(2,1)S(1)}, bf16[2,4,64]{2,1,0:T(4,128)(2,1)}, u32[]{:S(2)}) copy-start(bf16[2,4,64]{2,1,0:T(4,128)(2,1)} %param.29) | copy-start | bytes 3076
  90.2 10.5 %copy-start.47 = (bf16[2,48,3,64]{3,1,2,0:T(8,128)(2,1)S(1)}, bf16[2,48,3,64]{3,1,2,0:T(8,128)(2,1)}, u32[]{:S(2)}) copy-start(bf16[2,48,3,64]{3,1,2,0:T(8,128)(2,1)} %param.36) | copy-start | bytes 110596
  90.2 72.1 %all-to-all-start.1 = ((bf16[64,4,5418]{2,1,0:T(4,128)(2,1)}), bf16[64,4,5418]{2,1,0:T(4,128)(2,1)}, u32[]{:S(2)}, u32[]{:S(2)}) async-start(bf16[64,4,5418]{2,1,0:T(4,128)(2,1)} %stack.56), calls=%async_computation.1 | async-start | bytes 5636096 | tf_op jit(solution)/shard_map/all_to_all | solution.py:15
  96.7 296.1 %all-reduce.3.cloned.1.call-start = ((), (), s32[]{:S(2)}) async-start(), calls=%async_computation.2 | async-start | bytes 7864320 | tf_op jit(solution)/shard_map/psum | solution.py:171
  104.7 92.7 %copy-start.9 = (bf16[48,8,1,1,64]{4,3,1,0,2:T(2,128)(2,1)}, bf16[48,8,1,1,64]{4,3,1,0,2:T(2,128)(2,1)S(1)}, u32[]{:S(2)}) copy-start(bf16[48,8,1,1,64]{4,3,1,0,2:T(2,128)(2,1)S(1)} %get-tuple-element.155) | copy-start | bytes 147460
  109.4 72.5 %copy-start.62 = (f32[48]{0:T(128)}, f32[48]{0:T(128)S(1)}, u32[]{:S(2)}) copy-start(f32[48]{0:T(128)S(1)} %get-tuple-element.57) | copy-start | bytes 580
  109.4 78.5 %copy-start.54 = (f32[48]{0:T(128)}, f32[48]{0:T(128)S(1)}, u32[]{:S(2)}) copy-start(f32[48]{0:T(128)S(1)} %get-tuple-element.58) | copy-start | bytes 580
  110.3 71.6 %copy-start.36 = (f32[48,64]{1,0:T(8,128)}, f32[48,64]{1,0:T(8,128)S(1)}, u32[]{:S(2)}) copy-start(f32[48,64]{1,0:T(8,128)S(1)} %get-tuple-element.176) | copy-start | bytes 36868
  110.3 81.0 %copy-start.33 = (f32[48,64]{1,0:T(8,128)}, f32[48,64]{1,0:T(8,128)S(1)}, u32[]{:S(2)}) copy-start(f32[48,64]{1,0:T(8,128)S(1)} %get-tuple-element.173) | copy-start | bytes 36868
  110.3 81.1 %copy-start.34 = (f32[48,64]{1,0:T(8,128)}, f32[48,64]{1,0:T(8,128)S(1)}, u32[]{:S(2)}) copy-start(f32[48,64]{1,0:T(8,128)S(1)} %get-tuple-element.174) | copy-start | bytes 36868
  110.3 81.1 %copy-start.35 = (f32[48,64]{1,0:T(8,128)}, f32[48,64]{1,0:T(8,128)S(1)}, u32[]{:S(2)}) copy-start(f32[48,64]{1,0:T(8,128)S(1)} %get-tuple-element.175) | copy-start | bytes 36868
  181.8 9.5 %copy-start.27 = (f32[48,1,128]{2,1,0:T(1,128)}, f32[48,1,128]{2,1,0:T(1,128)S(1)}, u32[]{:S(2)}) copy-start(f32[48,1,128]{2,1,0:T(1,128)S(1)} %get-tuple-element.161) | copy-start | bytes 73732
  181.9 9.5 %copy-start.28 = (f32[48,1,128]{2,1,0:T(1,128)}, f32[48,1,128]{2,1,0:T(1,128)S(1)}, u32[]{:S(2)}) copy-start(f32[48,1,128]{2,1,0:T(1,128)S(1)} %get-tuple-element.162) | copy-start | bytes 73732
  189.5 7.9 %copy-start.80 = (f32[64]{0:T(128)S(1)}, f32[64]{0:T(128)}, u32[]{:S(2)}) copy-start(f32[64]{0:T(128)} %get-tuple-element.208) | copy-start | bytes 772
  189.5 8.0 %copy-start.16 = (bf16[2,64,2560]{2,1,0:T(8,128)(2,1)S(1)}, bf16[2,64,2560]{2,1,0:T(8,128)(2,1)}, u32[]{:S(2)}) copy-start(bf16[2,64,2560]{2,1,0:T(8,128)(2,1)} %param.34) | copy-start | bytes 1966084
  200.1 430.6 %all-reduce.5.cloned.1.call-start = ((), (), s32[]{:S(2)}) async-start(), calls=%async_computation.3 | async-start | bytes 7864320 | tf_op jit(solution)/shard_map/psum | solution.py:171
  203.6 135.5 %copy-start.1 = (f32[2,48,1,64,128]{4,3,2,1,0:T(8,128)S(1)}, f32[2,48,1,64,128]{4,3,2,1,0:T(8,128)}, u32[]{:S(2)}) copy-start(f32[2,48,1,64,128]{4,3,2,1,0:T(8,128)} %param.35) | copy-start | bytes 9437188
  348.1 48.8 %copy-start.51 = (f32[2560]{0:T(1024)S(1)}, f32[2560]{0:T(1024)}, u32[]{:S(2)}) copy-start(f32[2560]{0:T(1024)} %get-tuple-element.70) | copy-start | bytes 30724
  415.2 7.0 %copy-start.23 = (f32[48,1,128]{2,1,0:T(1,128)}, f32[48,1,128]{2,1,0:T(1,128)S(1)}, u32[]{:S(2)}) copy-start(f32[48,1,128]{2,1,0:T(1,128)S(1)} %get-tuple-element.137) | copy-start | bytes 73732
  415.2 7.0 %copy-start.24 = (f32[48,1,128]{2,1,0:T(1,128)}, f32[48,1,128]{2,1,0:T(1,128)S(1)}, u32[]{:S(2)}) copy-start(f32[48,1,128]{2,1,0:T(1,128)S(1)} %get-tuple-element.141) | copy-start | bytes 73732
  415.2 7.0 %copy-start.25 = (f32[48,1,128]{2,1,0:T(1,128)}, f32[48,1,128]{2,1,0:T(1,128)S(1)}, u32[]{:S(2)}) copy-start(f32[48,1,128]{2,1,0:T(1,128)S(1)} %get-tuple-element.143) | copy-start | bytes 73732
  415.3 7.0 %copy-start.26 = (f32[48,1,128]{2,1,0:T(1,128)}, f32[48,1,128]{2,1,0:T(1,128)S(1)}, u32[]{:S(2)}) copy-start(f32[48,1,128]{2,1,0:T(1,128)S(1)} %get-tuple-element.144) | copy-start | bytes 73732
  415.3 11.2 %copy-start.21 = (f32[48,1,128]{2,1,0:T(1,128)}, f32[48,1,128]{2,1,0:T(1,128)S(1)}, u32[]{:S(2)}) copy-start(f32[48,1,128]{2,1,0:T(1,128)S(1)} %get-tuple-element.134) | copy-start | bytes 73732
  415.3 11.2 %copy-start.22 = (f32[48,1,128]{2,1,0:T(1,128)}, f32[48,1,128]{2,1,0:T(1,128)S(1)}, u32[]{:S(2)}) copy-start(f32[48,1,128]{2,1,0:T(1,128)S(1)} %get-tuple-element.135) | copy-start | bytes 73732
  416.5 10.0 %copy-start.73 = (f32[48]{0:T(128)}, f32[48]{0:T(128)S(1)}, u32[]{:S(2)}) copy-start(f32[48]{0:T(128)S(1)} %get-tuple-element.237) | copy-start | bytes 580
  416.5 10.0 %copy-start.74 = (f32[48]{0:T(128)}, f32[48]{0:T(128)S(1)}, u32[]{:S(2)}) copy-start(f32[48]{0:T(128)S(1)} %get-tuple-element.238) | copy-start | bytes 580
  416.5 10.0 %copy-start.75 = (f32[48]{0:T(128)}, f32[48]{0:T(128)S(1)}, u32[]{:S(2)}) copy-start(f32[48]{0:T(128)S(1)} %get-tuple-element.239) | copy-start | bytes 580
  417.3 9.2 %copy-start.40 = (f32[48,64]{1,0:T(8,128)}, f32[48,64]{1,0:T(8,128)S(1)}, u32[]{:S(2)}) copy-start(f32[48,64]{1,0:T(8,128)S(1)} %bitcast_multiply_fusion.2) | copy-start | bytes 36868
  417.5 9.0 %copy-start.41 = (f32[48,64]{1,0:T(8,128)}, f32[48,64]{1,0:T(8,128)S(1)}, u32[]{:S(2)}) copy-start(f32[48,64]{1,0:T(8,128)S(1)} %get-tuple-element.146) | copy-start | bytes 36868
  417.5 9.0 %copy-start.42 = (f32[48,64]{1,0:T(8,128)}, f32[48,64]{1,0:T(8,128)S(1)}, u32[]{:S(2)}) copy-start(f32[48,64]{1,0:T(8,128)S(1)} %get-tuple-element.147) | copy-start | bytes 36868
  424.6 9.4 %copy-start.10 = (bf16[48,8,1,1,64]{4,3,1,0,2:T(2,128)(2,1)S(1)}, bf16[48,8,1,1,64]{4,3,1,0,2:T(2,128)(2,1)}, u32[]{:S(2)}) copy-start(bf16[48,8,1,1,64]{4,3,1,0,2:T(2,128)(2,1)} %get-tuple-element.128) | copy-start | bytes 147460
  424.6 9.4 %copy-start.79 = (f32[64]{0:T(128)S(1)}, f32[64]{0:T(128)}, u32[]{:S(2)}) copy-start(f32[64]{0:T(128)} %get-tuple-element.207) | copy-start | bytes 772
  424.6 9.4 %copy-start.17 = (bf16[2,64,2560]{2,1,0:T(8,128)(2,1)S(1)}, bf16[2,64,2560]{2,1,0:T(8,128)(2,1)}, u32[]{:S(2)}) copy-start(bf16[2,64,2560]{2,1,0:T(8,128)(2,1)} %param.34) | copy-start | bytes 1966084
  436.6 139.3 %copy-start.18 = (bf16[48,3,64]{2,0,1:T(8,128)(2,1)S(1)}, bf16[48,3,64]{2,0,1:T(8,128)(2,1)}, u32[]{:S(2)}) copy-start(bf16[48,3,64]{2,0,1:T(8,128)(2,1)} %get-tuple-element.181) | copy-start | bytes 55300
  436.7 139.2 %copy-start.6 = (bf16[48,8,1,1,64]{4,0,1,3,2:T(8,128)(2,1)S(1)}, bf16[48,8,1,1,64]{4,0,1,3,2:T(8,128)(2,1)}, u32[]{:S(2)}) copy-start(bf16[48,8,1,1,64]{4,0,1,3,2:T(8,128)(2,1)} %copy-done.5) | copy-start | bytes 147460
  578.1 8.3 %copy-start.4 = (f32[1,48,1,64,128]{4,3,2,1,0:T(8,128)S(1)}, f32[1,48,1,64,128]{4,3,2,1,0:T(8,128)}, u32[]{:S(2)}) copy-start(f32[1,48,1,64,128]{4,3,2,1,0:T(8,128)} %select_select_fusion.1) | copy-start | bytes 4718596
  (50 other events, 168.0 us)
Sparse Core Ops, SparseCore 0:
  200.2 192.4 all-reduce.2
  436.8 193.9 all-reduce.4
